TPU v7x, 32 devices: a whole 2x2x4 slice. The times are simulated.
32 devices in a mesh: row: 4 (over z), col: 8 (over y, x, core).
Axes of the slice: x: 2, y: 2, z: 4, core: 2. Of those that a mesh axis runs over, the one named last changes fastest.
Arguments:
- right_side: float32 [512, 512, 512], P(('row', 'col')), may hold values from -51 to 51
- coupling: float32 [512, 512, 512], P(('row', 'col')), may hold values from 0.01 to 0.3
Outputs:
- solution: float32 [512, 512, 512], P(('row', 'col'))
- residual: float32 [512, 512, 512], P(('row', 'col'))
- residual_norm: float32 [1], replicated
All inputs are finite; a program needn't handle non-finite values.
Results may differ from a plain program's by a relative error of at most 0.0003.
Values sent between devices are 32-bit elements; how exact they have to be, the bound alone decides.
A program may use at most 192 MiB of HBM per device.

v0:
```python
import math

import jax
import jax.numpy as jnp
from jax import lax
from jax.sharding import PartitionSpec as P

HIGHEST = lax.Precision.HIGHEST


def extended(block, sides, width):
    for axis, dim in sides:
        count = lax.axis_size(axis)
        forward = [(i, i + 1) for i in range(count - 1)]
        forward.append((count - 1, 0))
        backward = [(target, source) for source, target in forward]
        low = lax.ppermute(
            lax.slice_in_dim(block, block.shape[dim] - width, None, axis=dim), axis, forward
        )
        high = lax.ppermute(lax.slice_in_dim(block, 0, width, axis=dim), axis, backward)
        block = jnp.concatenate([low, block, high], axis=dim)
    return block


def cas_table(count):
    index = jnp.arange(count, dtype=jnp.int32)
    product = index[:, None] * index[None, :] % count
    angle = product.astype(jnp.float32) * (2.0 * math.pi / count)
    return jnp.cos(angle) + jnp.sin(angle)


def wave_square(count):
    index = jnp.arange(count, dtype=jnp.int32)
    signed = jnp.where(2 * index < count, index, index - count).astype(jnp.float32)
    return jnp.square(signed * (2.0 * math.pi / count))


def along_last(field, table):
    return jnp.einsum("abx,xk->abk", field, table, precision=HIGHEST)


def along_middle(field, table):
    return jnp.einsum("ayb,yk->akb", field, table, precision=HIGHEST)


def along_first(field, table):
    return jnp.einsum("zab,zk->kab", field, table, precision=HIGHEST)


def shards(right_side, coupling):
    planes, rows, cols = right_side.shape
    depth = planes * lax.axis_size("row") * lax.axis_size("col")
    table_x = cas_table(cols)
    table_y = cas_table(rows)
    table_z = cas_table(depth)
    spectra = along_middle(along_last(right_side, table_x), table_y)
    pencil = lax.all_to_all(spectra, ("row", "col"), split_axis=1, concat_axis=0, tiled=True)
    block = lax.axis_index(("row", "col"))
    width = pencil.shape[1]
    spectrum = along_first(pencil, table_z)
    start = block * width
    wave_rows = lax.dynamic_slice_in_dim(wave_square(rows), start, width, 0)
    eigen = (
        wave_square(depth)[:, None, None]
        + wave_rows[None, :, None]
        + wave_square(cols)[None, None, :]
    )
    volume = float(depth * rows * cols)
    positive = eigen > 0
    scaled = jnp.where(positive, spectrum / jnp.where(positive, eigen * volume, 1.0), 0.0)
    lines = along_first(scaled, table_z)
    slab = lax.all_to_all(lines, ("row", "col"), split_axis=0, concat_axis=1, tiled=True)
    slab = along_middle(slab, table_y)
    solution = along_last(slab, table_x)
    padded = extended(solution, ((("row", "col"), 0),), 1)
    lap = 6.0 * solution - padded[2:] - padded[:-2]
    lap = lap - jnp.roll(solution, 1, 1) - jnp.roll(solution, -1, 1)
    lap = lap - jnp.roll(solution, 1, 2) - jnp.roll(solution, -1, 2)
    residual = right_side - (coupling * solution + lap)
    squares = lax.psum(jnp.sum(residual * residual), ("row", "col"))
    residual_norm = jnp.sqrt(squares).reshape(1)
    return (solution, residual, residual_norm)


def solution(mesh):
    in_specs = (P(("row", "col"), None, None), P(("row", "col"), None, None))
    out_specs = (P(("row", "col"), None, None), P(("row", "col"), None, None), P())
    return jax.shard_map(shards, mesh=mesh, in_specs=in_specs, out_specs=out_specs, check_vma=False)
```

profile of v0, /device:TPU:14, one launch (start us, length us, event | category | flops | bytes accessed | tf_op | source)
XLA Modules:
  0.0 1289.1 jit_solution(7548929516048661643)
XLA Ops:
  0.6 68.0 %fusion.31 = f32[512,16,512]{2,0,1:T(8,128)} fusion(f32[16,512,512]{2,1,0:T(8,128)} %param.2), kind=kOutput, calls=%fused_computation.36 | convolution fusion | flops 25773735936 | bytes 33554432 | tf_op jit(solution)/shard_map/abx,xk->abk/dot_general | solution.py:39
  68.7 79.3 %fusion.19 = f32[16,512,512]{2,1,0:T(8,128)} fusion(f32[512,16,512]{2,0,1:T(8,128)} %fusion.31), kind=kOutput, calls=%fused_computation.23 | convolution fusion | flops 25773735936 | bytes 33554432 | tf_op jit(solution)/shard_map/ayb,yk->akb/dot_general | solution.py:43
  148.0 17.8 %copy.23 = f32[16,512,512]{2,0,1:T(8,128)} copy(f32[16,512,512]{2,1,0:T(8,128)} %fusion.19) | data formatting | bytes 33554432 | tf_op jit(solution)/shard_map/ayb,yk->akb/transpose | solution.py:43
  165.8 6.0 all-to-all-start
  171.8 0.1 dynamic_slice.3
  171.9 5.3 fusion.96
  177.2 5.3 fusion.94
  182.5 0.1 broadcast_add_fusion
  182.6 350.1 %all-to-all-done = f32[16,512,512]{2,0,1:T(8,128)} async-done(((f32[16,512,512]{2,0,1:T(8,128)}), f32[16,512,512]{2,0,1:T(8,128)}, u32[]{:S(2)}, u32[]{:S(2)}) %all-to-all-start) | async-done | bytes 16777248 | tf_op jit(solution)/shard_map/all_to_all | solution.py:57
  532.7 17.3 %copy.25 = f32[32,16,16,512]{3,2,1,0:T(8,128)S(1)} copy(f32[32,16,16,512]{3,1,2,0:T(8,128)} %bitcast.9) | data formatting | bytes 33554432 | tf_op jit(solution)/shard_map/all_to_all | solution.py:57
  550.1 79.4 %fusion.15 = f32[512,16,512]{2,0,1:T(8,128)S(1)} fusion(f32[512,16,512]{2,1,0:T(8,128)S(1)} %bitcast.54, f32[512,512,1]{1,0,2:T(8,128)} %fusion.94), kind=kOutput, calls=%fused_computation.19 | convolution fusion | flops 25769803776 | bytes 34603008 | tf_op jit(solution)/shard_map/zab,zk->kab/dot_general | solution.py:47
  629.4 40.3 %fusion.17 = f32[512,16,512]{2,0,1:T(8,128)} fusion(f32[512,16,512]{2,0,1:T(8,128)S(1)} %fusion.15, f32[512]{0:T(512)S(1)} %fusion.44, f32[512,16]{0,1:T(8,128)S(1)} %broadcast_add_fusion, f32[512,512,1]{1,0,2:T(8,128)} %fusion.96), kind=kOutput, calls=%fused_computation.22 | convolution fusion | flops 25794969600 | bytes 34637824 | tf_op jit(solution)/shard_map/zab,zk->kab/dot_general | solution.py:47
  669.8 17.9 %copy.29 = f32[512,16,512]{2,1,0:T(8,128)} copy(f32[512,16,512]{2,0,1:T(8,128)} %fusion.17) | data formatting | bytes 33554432 | tf_op jit(solution)/shard_map/zab,zk->kab/dot_general | solution.py:47
  687.7 15.5 %all-to-all-start.1 = ((f32[512,16,512]{2,1,0:T(8,128)}), f32[512,16,512]{2,1,0:T(8,128)}, u32[]{:S(2)}, u32[]{:S(2)}) async-start(f32[512,16,512]{2,1,0:T(8,128)} %copy.29), calls=%async_computation.1 | async-start | bytes 33554432 | tf_op jit(solution)/shard_map/all_to_all | solution.py:72
  703.2 4.1 fusion.92
  707.4 356.8 %all-to-all-done.1 = f32[512,16,512]{2,1,0:T(8,128)} async-done(((f32[512,16,512]{2,1,0:T(8,128)}), f32[512,16,512]{2,1,0:T(8,128)}, u32[]{:S(2)}, u32[]{:S(2)}) %all-to-all-start.1) | async-done | bytes 16777248 | tf_op jit(solution)/shard_map/all_to_all | solution.py:72
  1064.1 7.0 copy.30
  1071.2 42.4 %fusion.36 = f32[512,16,512]{2,0,1:T(8,128)} fusion(f32[16,512,512]{2,1,0:T(8,128)S(1)} %bitcast.53), kind=kOutput, calls=%fused_computation.41 | convolution fusion | flops 25773735936 | bytes 33554432 | tf_op jit(solution)/shard_map/ayb,yk->akb/dot_general | solution.py:43
  1113.6 31.4 %fusion.11 = f32[16,512,512]{2,1,0:T(8,128)S(1)} fusion(f32[512,16,512]{2,0,1:T(8,128)} %fusion.36, f32[512,512,1]{1,0,2:T(8,128)S(1)} %fusion.92), kind=kOutput, calls=%fused_computation.15 | convolution fusion | flops 25769803776 | bytes 34603008 | tf_op jit(solution)/shard_map/abx,xk->abk/dot_general | solution.py:39
  1145.0 0.0 copy-start
  1145.0 1.6 fusion.73
  1146.6 12.9 %fusion.75 = (f32[16,511,512]{2,1,0:T(8,128)}, f32[16,511,512]{2,1,0:T(8,128)}) fusion(f32[16,512,512]{2,1,0:T(8,128)S(1)} %fusion.11), kind=kLoop, calls=%fused_computation.84 | loop fusion | bytes 66977792 | tf_op jit(solution)/shard_map/jit(_roll_static)/slice | solution.py:77
  1159.5 0.0 collective-permute-start
  1159.5 0.5 collective-permute-start.1
  1160.0 12.7 fusion.77
  1172.7 0.1 fusion.74
  1172.8 0.0 copy-done
  1172.8 3.6 fusion.76
  1176.4 7.0 collective-permute-done
  1183.4 1.3 collective-permute-done.1
  1184.7 55.6 %multiply_reduce_fusion = (f32[]{:T(128)}, f32[16,512,512]{2,1,0:T(8,128)}) fusion(f32[16,512,512]{2,1,0:T(8,128)} %param.2, f32[16,512,1]{2,1,0:T(8,128)} %get-tuple-element.12, f32[16,512,511]{2,1,0:T(8,128)} %get-tuple-element.14, f32[16,512,511]{2,1,0:T(8,128)} %get-tuple-element.13, f32[16,512,1]{2,1,0:T(8,128)S(1)} %get-tuple-element.11, ...), kind=kLoop, calls=%fused_computation.21 | loop fusion | flops 75497472 | bytes 136314880 | tf_op jit(solution)/shard_map/reduce_sum | solution.py:80
  1240.3 46.4 %psum.7 = f32[]{:T(128)} all-reduce(f32[]{:T(128)} %get-tuple-element.3), channel_id=1, replica_groups=mesh['row'=4,'col'=8] {'row','col'}, use_global_device_ids=true, to_apply=%region_1.2 | all-reduce | flops 1 | bytes 8 | tf_op jit(solution)/shard_map/psum | solution.py:80
  (1 shorter events, 0.0 us)
Async XLA Ops:
  165.8 366.9 %all-to-all-start = ((f32[16,512,512]{2,0,1:T(8,128)}), f32[16,512,512]{2,0,1:T(8,128)}, u32[]{:S(2)}, u32[]{:S(2)}) async-start(f32[16,512,512]{2,0,1:T(8,128)} %copy.23), calls=%async_computation | async-start | bytes 33554432 | tf_op jit(solution)/shard_map/all_to_all | solution.py:57
  687.7 376.5 %all-to-all-start.1 = ((f32[512,16,512]{2,1,0:T(8,128)}), f32[512,16,512]{2,1,0:T(8,128)}, u32[]{:S(2)}, u32[]{:S(2)}) async-start(f32[512,16,512]{2,1,0:T(8,128)} %copy.29), calls=%async_computation.1 | async-start | bytes 33554432 | tf_op jit(solution)/shard_map/all_to_all | solution.py:72
  1145.0 27.8 %copy-start = (f32[16,512,512]{2,1,0:T(8,128)}, f32[16,512,512]{2,1,0:T(8,128)S(1)}, u32[]{:S(2)}) copy-start(f32[16,512,512]{2,1,0:T(8,128)S(1)} %fusion.11) | copy-start | bytes 50331652
  1159.5 23.9 %collective-permute-start = (f32[1,512,512]{2,1,0:T(8,128)}, f32[1,512,512]{2,1,0:T(8,128)S(1)}, u32[]{:S(2)}, u32[]{:S(2)}) collective-permute-start(f32[1,512,512]{2,1,0:T(8,128)} %get-tuple-element.5), channel_id=1, source_target_pairs={{1,0},{2,1},{3,2},{4,3},{5,4},{6,5},{7,6},{8,7},{9,8},{10,9},{11,1... | collective-permute-start | bytes 3145736 | tf_op jit(solution)/shard_map/ppermute | solution.py:20
  1159.5 25.1 %collective-permute-start.1 = (f32[1,512,512]{2,1,0:T(8,128)}, f32[1,512,512]{2,1,0:T(8,128)}, u32[]{:S(2)}, u32[]{:S(2)}) collective-permute-start(f32[1,512,512]{2,1,0:T(8,128)} %get-tuple-element.6), channel_id=1, source_target_pairs={{0,1},{1,2},{2,3},{3,4},{4,5},{5,6},{6,7},{7,8},{8,9},{9,10},{10,1... | collective-permute-start | bytes 3145736 | tf_op jit(solution)/shard_map/ppermute | solution.py:17
where the time goes:
time: 1300 us; the launch traced here: 1290 us
  waiting for transfers between devices  715 us (55%)
  matrix products  341 us (26%)
  local copies, waits for them, and re-layouts  91 us (7%)
  other arithmetic  70.5 us (5%)
  blocking collectives  46.4 us (4%)
  starting transfers between devices  22.1 us (2%)
    all_to_all x1, waiting for transfers between devices, shards(): lax.all_to_all(lines, ('row', 'col'), split_axis=0, concat_axis=1, tiled=...  357 us
    all_to_all x1, waiting for transfers between devices, shards(): lax.all_to_all(spectra, ('row', 'col'), split_axis=1, concat_axis=0, tile...  350 us
    dot_general x2, matrix products, along_middle(): return jnp.einsum('ayb,yk->akb', field, table, precision=HIGHEST)  122 us
    dot_general x2, matrix products, along_first(): return jnp.einsum('zab,zk->kab', field, table, precision=HIGHEST)  120 us
    dot_general x2, matrix products, along_last(): return jnp.einsum('abx,xk->abk', field, table, precision=HIGHEST)  99.4 us
    reduce_sum x1, other arithmetic, shards(): squares = lax.psum(jnp.sum(residual * residual), ('row', 'col'))  55.6 us
    psum x1, blocking collectives, shards(): squares = lax.psum(jnp.sum(residual * residual), ('row', 'col'))  46.4 us
  transfers between devices with their start and end apart: 4, of which 4 were waited for; matrix products, arithmetic and copies ran while one was open for 2% of the time, Pallas kernels for 0%

commit v1 on v0

v1 whole, which is shorter than its diff:
```python
import functools
import math

import jax
import jax.numpy as jnp
from jax import lax
from jax.experimental import pallas as pl
from jax.experimental.pallas import tpu as pltpu
from jax.sharding import PartitionSpec as P

HIGH = lax.Precision.HIGH
AXES = ("row", "col")
CHUNKS = 2


def half_tables(count):
    half = count // 2
    index = jnp.arange(half, dtype=jnp.int32)

    def table(frequency):
        product = index[:, None] * frequency[None, :] % count
        angle = product.astype(jnp.float32) * (2.0 * math.pi / count)
        return jnp.cos(angle) + jnp.sin(angle)

    return table(2 * index), table(2 * index + 1)


def wave_square(count):
    half = count // 2
    even = 2 * jnp.arange(half, dtype=jnp.int32)
    index = jnp.concatenate([even, even + 1])
    signed = jnp.where(2 * index < count, index, index - count).astype(jnp.float32)
    return jnp.square(signed * (2.0 * math.pi / count))


LETTERS = ("jbc,jk->kbc", "ajc,jk->akc", "abj,jk->abk")
BACK = ("kbc,jk->jbc", "akc,jk->ajc", "abk,jk->abj")


def halves(field, dim):
    half = field.shape[dim] // 2
    return (
        lax.slice_in_dim(field, 0, half, axis=dim),
        lax.slice_in_dim(field, half, None, axis=dim),
    )


def dot(spec, field, table):
    return jnp.einsum(spec, field, table, precision=HIGH)


def forward(field, tables, dim):
    low, high = halves(field, dim)
    even = dot(LETTERS[dim], low + high, tables[0])
    odd = dot(LETTERS[dim], low - high, tables[1])
    return jnp.concatenate([even, odd], axis=dim)


def inverse(spectrum, tables, dim):
    low, high = halves(spectrum, dim)
    even = dot(BACK[dim], low, tables[0])
    odd = dot(BACK[dim], high, tables[1])
    return jnp.concatenate([even + odd, even - odd], axis=dim)


def split(value):
    high = value.astype(jnp.bfloat16)
    low = (value - high.astype(jnp.float32)).astype(jnp.bfloat16)
    return high, low


def tail_kernel(
    count, per, *refs
):
    slabs, refs = refs[:2 * per], refs[2 * per:]
    below, above, even_ref, odd_ref, right_ref, coupling_ref = refs[:6]
    solution_ref, residual_ref, squares_ref, tables, ring = refs[6:]
    step = pl.program_id(0)

    @pl.when(step == 0)
    def _():
        for which, ref in enumerate((even_ref, odd_ref)):
            high, low = split(ref[...])
            tables[2 * which] = high
            tables[2 * which + 1] = low
        squares_ref[...] = jnp.zeros_like(squares_ref)

    def transform(value, which):
        high, low = split(value)
        total = jnp.dot(low, tables[2 * which], preferred_element_type=jnp.float32)
        total += jnp.dot(high, tables[2 * which + 1], preferred_element_type=jnp.float32)
        return total + jnp.dot(high, tables[2 * which], preferred_element_type=jnp.float32)

    def plane(even, odd):
        first = transform(even, 0)
        second = transform(odd, 1)
        half = first.shape[1]
        slot = ring.at[lax.rem(step, 3)]
        slot[:, :half] = first + second
        slot[:, half:] = first - second

    @pl.when(step == 0)
    def _():
        plane(below[0], below[1])

    @pl.when(step == count + 1)
    def _():
        plane(above[0], above[1])

    @pl.when((step > 0) & (step <= count))
    def _():
        parts = [ref[0] for ref in slabs]
        if per == 1:
            plane(parts[0], parts[1])
        else:
            plane(jnp.concatenate(parts[:per], axis=1), jnp.concatenate(parts[per:], axis=1))
        solution_ref[0] = ring[lax.rem(step, 3)]

    @pl.when(step > 1)
    def _():
        here = ring[lax.rem(step - 1, 3)]
        rows, cols = here.shape
        lap = 6.0 * here - ring[lax.rem(step, 3)] - ring[lax.rem(step - 2, 3)]
        lap = lap - pltpu.roll(here, 1, 0) - pltpu.roll(here, rows - 1, 0)
        lap = lap - pltpu.roll(here, 1, 1) - pltpu.roll(here, cols - 1, 1)
        residual = right_ref[0] - (coupling_ref[0] * here + lap)
        residual_ref[0] = residual
        squares_ref[...] += jnp.sum(residual * residual, axis=0, keepdims=True)


def tail(slabs, below, above, tables, right_side, coupling):
    planes, rows, cols = right_side.shape
    per = len(slabs) // 2

    def clip(shift):
        return lambda t: (jnp.clip(t - shift, 0, planes - 1), 0, 0)

    def whole(shape):
        return pl.BlockSpec(shape, lambda t: (0,) * len(shape))

    block = (1, rows, cols)
    return pl.pallas_call(
        functools.partial(tail_kernel, planes, per),
        grid=(planes + 2,),
        in_specs=[pl.BlockSpec((1, rows, part.shape[2]), clip(1)) for part in slabs]
        + [whole(below.shape), whole(above.shape), whole(tables[0].shape), whole(tables[1].shape)]
        + [pl.BlockSpec(block, clip(2)), pl.BlockSpec(block, clip(2))],
        out_specs=[pl.BlockSpec(block, clip(1)), pl.BlockSpec(block, clip(2)), whole((1, cols))],
        out_shape=[
            jax.ShapeDtypeStruct(right_side.shape, jnp.float32),
            jax.ShapeDtypeStruct(right_side.shape, jnp.float32),
            jax.ShapeDtypeStruct((1, cols), jnp.float32),
        ],
        scratch_shapes=[
            pltpu.VMEM((4,) + tables[0].shape, jnp.bfloat16),
            pltpu.VMEM((3, rows, cols), jnp.float32),
        ],
        compiler_params=pltpu.CompilerParams(vmem_limit_bytes=48 * 1024 * 1024),
        name="tail",
    )(*slabs, below, above, tables[0], tables[1], right_side, coupling)


def twice(left, right):
    total = jnp.dot(left[1], right[0], preferred_element_type=jnp.float32)
    total += jnp.dot(left[0], right[1], preferred_element_type=jnp.float32)
    return total + jnp.dot(left[0], right[0], preferred_element_type=jnp.float32)


def keep(tables, refs):
    for position, ref in enumerate(refs):
        high, low = split(ref[...])
        tables[2 * position] = high
        tables[2 * position + 1] = low


def pair(tables, position):
    return tables[2 * position], tables[2 * position + 1]


def plane_kernel(sign, right_ref, x_ref, even_ref, odd_ref, out_ref, x_table, y_tables):
    @pl.when(pl.program_id(0) == 0)
    def _():
        keep(x_table, (x_ref,))
        keep(y_tables, (even_ref, odd_ref))

    field = right_ref[0]
    rows, cols = field.shape
    lines = twice(split(field[:, :cols // 2] + sign * field[:, cols // 2:]), pair(x_table, 0))
    low, high = lines[:rows // 2], lines[rows // 2:]
    ranks, _, width, half = out_ref.shape
    shape = (ranks // 2, width, half)
    out_ref[:ranks // 2, 0] = twice(pair(y_tables, 0), split(low + high)).reshape(shape)
    out_ref[ranks // 2:, 0] = twice(pair(y_tables, 1), split(low - high)).reshape(shape)


def whole(shape):
    return pl.BlockSpec(shape, lambda *_: (0,) * len(shape))


LIMIT = pltpu.CompilerParams(vmem_limit_bytes=56 * 1024 * 1024)


def planes_forward(right_side, sign, table_x, tables_y, ranks):
    planes, rows, cols = right_side.shape
    width, half = rows // ranks, cols // 2
    return pl.pallas_call(
        functools.partial(plane_kernel, sign),
        grid=(planes,),
        in_specs=[pl.BlockSpec((1, rows, cols), lambda t: (t, 0, 0)), whole(table_x.shape)]
        + [whole(table.shape) for table in tables_y],
        out_specs=pl.BlockSpec((ranks, 1, width, half), lambda t: (0, t, 0, 0)),
        out_shape=jax.ShapeDtypeStruct((ranks, planes, width, half), jnp.float32),
        scratch_shapes=[
            pltpu.VMEM((2,) + table_x.shape, jnp.bfloat16),
            pltpu.VMEM((4,) + tables_y[0].shape, jnp.bfloat16),
        ],
        compiler_params=LIMIT,
        cost_estimate=pl.CostEstimate(
            flops=12 * planes * rows * half * half,
            bytes_accessed=6 * planes * rows * cols, transcendentals=0,
        ),
        name="planes_forward",
    )(right_side, table_x, *tables_y)


def line_kernel(volume, pencil_ref, rows_ref, z_ref, x_ref, *refs):
    *table_refs, out_ref, tables = refs
    lane = pl.program_id(1)

    @pl.when((lane == 0) & (pl.program_id(0) == 0))
    def _():
        keep(tables, table_refs)

    depth, group, span = pencil_ref.shape
    half = depth // 2
    source = pencil_ref.reshape(depth * group, span)
    target = out_ref.reshape(depth * group, span)

    def scale(spectrum, wave_z, row):
        eigen = wave_z + row + x_ref[...]
        positive = eigen > 0
        return jnp.where(positive, spectrum / jnp.where(positive, eigen * volume, 1.0), 0.0)

    def body(index, carry):
        low = source[pl.ds(index, half, stride=group), :]
        high = source[pl.ds(index + half * group, half, stride=group), :]
        row = rows_ref[pl.program_id(0) * group + index]
        even = scale(twice(pair(tables, 0), split(low + high)), z_ref[:half], row)
        odd = scale(twice(pair(tables, 1), split(low - high)), z_ref[half:], row)
        first = twice(pair(tables, 2), split(even))
        second = twice(pair(tables, 3), split(odd))
        target[pl.ds(index, half, stride=group), :] = first + second
        target[pl.ds(index + half * group, half, stride=group), :] = first - second
        return carry

    lax.fori_loop(0, group, body, 0)


def lines_solved(pencil, wave_rows, wave_z, wave_x, tables, volume):
    depth, width, span = pencil.shape
    group, lanes = 8, 128
    transposed = (tables[0].T, tables[1].T) + tuple(tables)
    block = pl.BlockSpec((depth, group, lanes), lambda y, x: (0, y, x))
    return pl.pallas_call(
        functools.partial(line_kernel, volume),
        grid=(width // group, span // lanes),
        in_specs=[
            block,
            pl.BlockSpec(memory_space=pltpu.SMEM),
            whole((depth, 1)),
            pl.BlockSpec((1, lanes), lambda y, x: (0, x)),
        ]
        + [whole(table.shape) for table in transposed],
        out_specs=block,
        out_shape=jax.ShapeDtypeStruct(pencil.shape, jnp.float32),
        scratch_shapes=[pltpu.VMEM((8,) + tables[0].shape, jnp.bfloat16)],
        compiler_params=LIMIT,
        cost_estimate=pl.CostEstimate(
            flops=12 * depth * width * span * depth,
            bytes_accessed=8 * depth * width * span, transcendentals=0,
        ),
        name="lines_solved",
    )(pencil, wave_rows, wave_z[:, None], wave_x[None], *transposed)


def shards(right_side, coupling):
    planes, rows, cols = right_side.shape
    ranks = lax.axis_size("row") * lax.axis_size("col")
    depth = planes * ranks
    tables_x = half_tables(cols)
    tables_y = half_tables(rows)
    tables_z = half_tables(depth)
    block = lax.axis_index(AXES)
    width = rows // ranks
    wave_rows = lax.dynamic_slice_in_dim(wave_square(rows), block * width, width, 0)
    wave_z = wave_square(depth)
    wave_x = wave_square(cols)
    volume = float(depth * rows * cols)

    low, high = halves(right_side, 2)
    parts = (low + high, low - high)
    span = cols // CHUNKS
    per = CHUNKS // 2
    slabs = []
    for chunk in range(CHUNKS):
        which, piece = divmod(chunk, per)
        columns = tables_x[which][:, piece * span:(piece + 1) * span]
        waves = wave_x[chunk * span:(chunk + 1) * span]
        if width % 8 == 0:
            sides = (tables_y[0].T, tables_y[1].T)
            spectra = planes_forward(right_side, 1.0 - 2.0 * which, columns, sides, ranks)
            pencil = lax.all_to_all(spectra, AXES, split_axis=0, concat_axis=0, tiled=True)
            pencil = pencil.reshape(depth, width, span)
            lines = lines_solved(pencil, wave_rows, wave_z, waves, tables_z, volume)
            lines = lines.reshape(ranks, planes, width, span)
            slab = lax.all_to_all(lines, AXES, split_axis=0, concat_axis=0, tiled=True)
            slab = slab.transpose(1, 0, 2, 3).reshape(planes, rows, span)
        else:
            spectra = forward(dot(LETTERS[2], parts[which], columns), tables_y, 1)
            pencil = lax.all_to_all(spectra, AXES, split_axis=1, concat_axis=0, tiled=True)
            spectrum = forward(pencil, tables_z, 0)
            eigen = wave_z[:, None, None] + wave_rows[None, :, None] + waves[None, None, :]
            positive = eigen > 0
            scaled = jnp.where(positive, spectrum / jnp.where(positive, eigen * volume, 1.0), 0.0)
            lines = inverse(scaled, tables_z, 0)
            slab = lax.all_to_all(lines, AXES, split_axis=0, concat_axis=1, tiled=True)
        slabs.append(inverse(slab, tables_y, 1))
    count = ranks
    ahead = [(i, (i + 1) % count) for i in range(count)]
    behind = [(target, source) for source, target in ahead]

    def edge(index, ring):
        parts = [lax.slice_in_dim(part, index, index + 1, axis=0) for part in slabs]
        even = jnp.concatenate(parts[:per], axis=2)
        odd = jnp.concatenate(parts[per:], axis=2)
        return lax.ppermute(jnp.concatenate([even, odd], axis=0), AXES, ring)

    below = edge(planes - 1, ahead)
    above = edge(0, behind)
    back = (tables_x[0].T, tables_x[1].T)
    answer, residual, partial = tail(slabs, below, above, back, right_side, coupling)
    squares = lax.psum(jnp.sum(partial), AXES)
    return (answer, residual, jnp.sqrt(squares).reshape(1))


def solution(mesh):
    spec = P(AXES, None, None)
    return jax.shard_map(
        shards, mesh=mesh, in_specs=(spec, spec), out_specs=(spec, spec, P()), check_vma=False
    )
```

time: 1300 us -> 916 us (0.70)
  matrix products: 341 us -> 19.2 us
  Pallas kernels: 0 us -> 136 us
  local copies, waits for them, and re-layouts: 91 us -> 17 us
  waiting for transfers between devices: 715 us -> 643 us
  other arithmetic: 70.5 us -> 18.5 us
    dot_general x6 -> x4, matrix products: 341 us -> 19.2 us  [dot(): return jnp.einsum(spec, field, table, precision=HIGH)]
    pallas_call x0 -> x5, Pallas kernels: none -> 136 us  [the longest x2 53.2 us: lines_solved(): pl.pallas_call(functools.partial(line_kernel, volume), grid=(width // gro...]
    all_to_all x2 -> x4, waiting for transfers between devices: 707 us -> 631 us  [the longest x2 321 us: shards(): slab = lax.all_to_all(lines, AXES, split_axis=0, concat_axis=0, tiled=True)]
    reduce_sum x1, other arithmetic: 55.6 us -> 0.6 us  [shards(): squares = lax.psum(jnp.sum(partial), AXES)]
    slice x5 -> x1, local copies, waits for them, and re-layouts: 30.9 us -> 0.6 us  [shards(): waves = wave_x[chunk * span:(chunk + 1) * span]]
    all_to_all x2 -> x0, local copies, waits for them, and re-layouts: 24.4 us -> none  [the longest x1 17.3 us: shards(): lax.all_to_all(spectra, ('row', 'col'), split_axis=1, concat_axis=0, tile...]
    dot_general x1 -> x0, local copies, waits for them, and re-layouts: 17.9 us -> none  [along_first(): return jnp.einsum('zab,zk->kab', field, table, precision=HIGHEST)]
    dot_general x3 -> x0, other arithmetic: 14.7 us -> none  [the longest x2 10.6 us: along_first(): return jnp.einsum('zab,zk->kab', field, table, precision=HIGHEST)]
  transfers between devices with their start and end apart: 4 -> 6, of which waited for: 4 -> 6; matrix products, arithmetic and copies ran while one was open for 2% -> 3% of each run, Pallas kernels for 0% -> 8%
where the time goes in v1:
time: 916 us; the launch traced here: 913 us
  waiting for transfers between devices  643 us (70%)
  Pallas kernels  136 us (15%)
  blocking collectives  42.7 us (5%)
  starting transfers between devices  34.3 us (4%)
  matrix products  19.2 us (2%)
  other arithmetic  18.5 us (2%)
  local copies, waits for them, and re-layouts  17 us (2%)
    all_to_all x2, waiting for transfers between devices, shards(): slab = lax.all_to_all(lines, AXES, split_axis=0, concat_axis=0, tiled=True)  321 us
    all_to_all x2, waiting for transfers between devices, shards(): lax.all_to_all(spectra, AXES, split_axis=0, concat_axis=0, tiled=True)  310 us
    pallas_call x2, Pallas kernels, lines_solved(): pl.pallas_call(functools.partial(line_kernel, volume), grid=(width // gro...  53.2 us
    pallas_call x2, Pallas kernels, planes_forward(): pl.pallas_call(functools.partial(plane_kernel, sign), grid=(planes,), in_...  45 us
    psum x1, blocking collectives, shards(): squares = lax.psum(jnp.sum(partial), AXES)  42.7 us
    pallas_call x1, Pallas kernels, tail(): pl.pallas_call(functools.partial(tail_kernel, planes, per), grid=(planes...  37.7 us
    dot_general x4, matrix products, dot(): return jnp.einsum(spec, field, table, precision=HIGH)  19.2 us
  transfers between devices with their start and end apart: 6, of which 6 were waited for; matrix products, arithmetic and copies ran while one was open for 3% of the time, Pallas kernels for 8%

profile of v1, /device:TPU:14, one launch (start us, length us, event | category | flops | bytes accessed | tf_op | source)
XLA Modules:
  0.0 913.1 jit_solution(908672655470041583)
XLA Ops:
  0.7 5.2 sine_add_fusion
  5.8 22.5 %planes_forward.3 = f32[32,16,16,256]{3,2,1,0:T(8,128)} custom-call(f32[16,512,512]{2,1,0:T(8,128)} %refs_6_.1, f32[256,256]{1,0:T(8,128)} %get-tuple-element.21.refs_3_.x_ref, f32[256,256]{1,0:T(8,128)} %get-tuple-element.26.even_ref.refs_0_.refs_4_, f32[256,256]{1,0:T(8,128)} %get-tuple-element.22.odd_ref.refs_1_.refs_5_), custom_call_target="tpu_custom_call" | custom-call | flops 6442450944 | bytes 25165824 | tf_op jit(solution)/shard_map/planes_forward/pallas_call | solution.py:206
  28.3 6.0 all-to-all-start.2
  34.3 22.5 %planes_forward.2 = f32[32,16,16,256]{3,2,1,0:T(8,128)} custom-call(f32[16,512,512]{2,1,0:T(8,128)} %refs_6_.1, f32[256,256]{1,0:T(8,128)} %get-tuple-element.25.x_ref.refs_2_, f32[256,256]{1,0:T(8,128)} %get-tuple-element.26.even_ref.refs_0_.refs_4_, f32[256,256]{1,0:T(8,128)} %get-tuple-element.22.odd_ref.refs_1_.refs_5_), custom_call_target="tpu_custom_call" | custom-call | flops 6442450944 | bytes 25165824 | tf_op jit(solution)/shard_map/planes_forward/pallas_call | solution.py:206
  56.8 158.4 %all-to-all-done.2 = f32[32,16,16,256]{3,2,1,0:T(8,128)} async-done(((f32[32,16,16,256]{3,2,1,0:T(8,128)}), f32[32,16,16,256]{3,2,1,0:T(8,128)}, u32[]{:S(2)}, u32[]{:S(2)}) %all-to-all-start.2) | async-done | bytes 8388640 | tf_op jit(solution)/shard_map/all_to_all | solution.py:312
  215.2 8.7 all-to-all-start
  225.0 0.6 fusion.59
  225.6 0.8 multiply_multiply_fusion.z_ref
  226.4 26.6 %lines_solved.3 = f32[512,16,256]{2,1,0:T(8,128)} custom-call(f32[512,16,256]{2,1,0:T(8,128)} %bitcast.11.pencil_ref, f32[16]{0:T(128)} %dynamic_slice.3.rows_ref, f32[512,1]{1,0:T(8,128)} %multiply_multiply_fusion.z_ref, f32[1,256]{1,0:T(1,128)} %bitcast.44, f32[256,256]{1,0:T(8,128)} %get-tuple-element.26.even_ref.refs_0_.refs_4_, ...), custom_call_target="tpu_custom_call" | custom-call | flops 12884901888 | bytes 16777216 | tf_op jit(solution)/shard_map/lines_solved/pallas_call | solution.py:264
  253.0 151.8 %all-to-all-done = f32[32,16,16,256]{3,2,1,0:T(8,128)} async-done(((f32[32,16,16,256]{3,2,1,0:T(8,128)}), f32[32,16,16,256]{3,2,1,0:T(8,128)}, u32[]{:S(2)}, u32[]{:S(2)}) %all-to-all-start) | async-done | bytes 8388640 | tf_op jit(solution)/shard_map/all_to_all | solution.py:312
  404.7 8.9 all-to-all-start.3
  413.6 26.6 %lines_solved.2 = f32[512,16,256]{2,1,0:T(8,128)} custom-call(f32[512,16,256]{2,1,0:T(8,128)} %bitcast.1.pencil_ref, f32[16]{0:T(128)} %dynamic_slice.3.rows_ref, f32[512,1]{1,0:T(8,128)} %multiply_multiply_fusion.z_ref, f32[1,256]{1,0:T(1,128)} %bitcast.43, f32[256,256]{1,0:T(8,128)} %get-tuple-element.26.even_ref.refs_0_.refs_4_, ...), custom_call_target="tpu_custom_call" | custom-call | flops 12884901888 | bytes 16777216 | tf_op jit(solution)/shard_map/lines_solved/pallas_call | solution.py:264
  440.2 154.2 %all-to-all-done.3 = f32[32,16,16,256]{3,2,1,0:T(8,128)} async-done(((f32[32,16,16,256]{3,2,1,0:T(8,128)}), f32[32,16,16,256]{3,2,1,0:T(8,128)}, u32[]{:S(2)}, u32[]{:S(2)}) %all-to-all-start.3) | async-done | bytes 8388640 | tf_op jit(solution)/shard_map/all_to_all | solution.py:316
  594.5 8.9 all-to-all-start.1
  603.3 4.4 copy.23
  607.7 3.4 fusion
  611.1 6.5 add_bitcast_fusion
  617.6 166.6 %all-to-all-done.1 = f32[32,16,16,256]{3,2,1,0:T(8,128)} async-done(((f32[32,16,16,256]{3,2,1,0:T(8,128)}), f32[32,16,16,256]{3,2,1,0:T(8,128)}, u32[]{:S(2)}, u32[]{:S(2)}) %all-to-all-start.1) | async-done | bytes 8388640 | tf_op jit(solution)/shard_map/all_to_all | solution.py:316
  784.2 4.4 copy.22
  788.6 3.4 copy-done.6
  792.0 3.4 fusion.4
  795.3 6.0 add_bitcast_fusion.1
  801.5 1.8 copy-done.4
  803.4 1.4 copy-done.5
  805.0 1.7 collective-permute-start.1
  806.7 4.2 pad_maximum_fusion.1.refs_1_
  810.9 7.5 pad_maximum_fusion.refs_0_
  818.4 10.5 %collective-permute-done.refs_2_ = f32[2,512,256]{2,1,0:T(8,128)S(1)} collective-permute-done((f32[2,512,256]{2,1,0:T(8,128)S(1)}, f32[2,512,256]{2,1,0:T(8,128)S(1)}, u32[]{:S(2)}, u32[]{:S(2)}) %collective-permute-start) | collective-permute-done | bytes 1048608 | tf_op jit(solution)/shard_map/ppermute | solution.py:336
  828.9 1.4 collective-permute-done.1.refs_3_
  830.3 37.7 %tail.1 = (f32[16,512,512]{2,1,0:T(8,128)}, f32[16,512,512]{2,1,0:T(8,128)}, f32[1,512]{1,0:T(1,128)S(1)}) custom-call(f32[16,512,256]{2,1,0:T(8,128)} %pad_maximum_fusion.refs_0_, f32[16,512,256]{2,1,0:T(8,128)} %pad_maximum_fusion.1.refs_1_, f32[2,512,256]{2,1,0:T(8,128)S(1)} %collective-permute-done.refs_2_, ...), custom_call_target="tpu_custom_call" | custom-call | tf_op jit(solution)/shard_map/tail/pallas_call | solution.py:142
  868.0 0.6 reduce_sum.9
  868.6 42.7 %psum.7 = f32[]{:T(128)} all-reduce(f32[]{:T(128)} %reduce_sum.9), channel_id=1, replica_groups=mesh['row'=4,'col'=8] {'row','col'}, use_global_device_ids=true, to_apply=%region_1.2 | all-reduce | flops 1 | bytes 8 | tf_op jit(solution)/shard_map/psum | solution.py:342
  (25 shorter events, 1.5 us)
Async XLA Ops:
  28.3 186.9 %all-to-all-start.2 = ((f32[32,16,16,256]{3,2,1,0:T(8,128)}), f32[32,16,16,256]{3,2,1,0:T(8,128)}, u32[]{:S(2)}, u32[]{:S(2)}) async-start(f32[32,16,16,256]{3,2,1,0:T(8,128)} %planes_forward.3), calls=%async_computation.2 | async-start | bytes 16777216 | tf_op jit(solution)/shard_map/all_to_all | solution.py:312
  215.2 189.5 %all-to-all-start = ((f32[32,16,16,256]{3,2,1,0:T(8,128)}), f32[32,16,16,256]{3,2,1,0:T(8,128)}, u32[]{:S(2)}, u32[]{:S(2)}) async-start(f32[32,16,16,256]{3,2,1,0:T(8,128)} %planes_forward.2), calls=%async_computation | async-start | bytes 16777216 | tf_op jit(solution)/shard_map/all_to_all | solution.py:312
  404.7 189.7 %all-to-all-start.3 = ((f32[32,16,16,256]{3,2,1,0:T(8,128)}), f32[32,16,16,256]{3,2,1,0:T(8,128)}, u32[]{:S(2)}, u32[]{:S(2)}) async-start(f32[32,16,16,256]{3,2,1,0:T(8,128)} %bitcast.40), calls=%async_computation.3 | async-start | bytes 16777216 | tf_op jit(solution)/shard_map/all_to_all | solution.py:316
  594.5 189.7 %all-to-all-start.1 = ((f32[32,16,16,256]{3,2,1,0:T(8,128)}), f32[32,16,16,256]{3,2,1,0:T(8,128)}, u32[]{:S(2)}, u32[]{:S(2)}) async-start(f32[32,16,16,256]{3,2,1,0:T(8,128)} %bitcast.39), calls=%async_computation.1 | async-start | bytes 16777216 | tf_op jit(solution)/shard_map/all_to_all | solution.py:316
  788.5 3.4 copy-start.6
  795.3 6.0 copy-start.2
  795.3 6.0 copy-start.3
  801.3 2.0 copy-start.4
  801.4 3.4 copy-start.5
  804.8 24.0 %collective-permute-start = (f32[2,512,256]{2,1,0:T(8,128)S(1)}, f32[2,512,256]{2,1,0:T(8,128)S(1)}, u32[]{:S(2)}, u32[]{:S(2)}) collective-permute-start(f32[2,512,256]{2,1,0:T(8,128)S(1)} %pad_maximum_fusion.2), channel_id=1, source_target_pairs={{0,1},{1,2},{2,3},{3,4},{4,5},{5,6},{6,7},{7,8},{8,9},{9,10},{10,1... | collective-permute-start | bytes 3145736 | tf_op jit(solution)/shard_map/ppermute | solution.py:336
  805.0 25.3 %collective-permute-start.1 = (f32[2,512,256]{2,1,0:T(8,128)S(1)}, f32[2,512,256]{2,1,0:T(8,128)S(1)}, u32[]{:S(2)}, u32[]{:S(2)}) collective-permute-start(f32[2,512,256]{2,1,0:T(8,128)S(1)} %pad_maximum_fusion.3), channel_id=1, source_target_pairs={{1,0},{2,1},{3,2},{4,3},{5,4},{6,5},{7,6},{8,7},{9,8},{10,9},{11,1... | collective-permute-start | bytes 3145736 | tf_op jit(solution)/shard_map/ppermute | solution.py:336
  810.9 19.4 %copy-start = (f32[256,256]{1,0:T(8,128)S(1)}, f32[256,256]{1,0:T(8,128)}, u32[]{:S(2)}) copy-start(f32[256,256]{1,0:T(8,128)} %get-tuple-element.22.odd_ref.refs_1_.refs_5_) | copy-start | bytes 786436
  810.9 19.4 %copy-start.1 = (f32[256,256]{1,0:T(8,128)S(1)}, f32[256,256]{1,0:T(8,128)}, u32[]{:S(2)}) copy-start(f32[256,256]{1,0:T(8,128)} %get-tuple-element.26.even_ref.refs_0_.refs_4_) | copy-start | bytes 786436
